TPU v7x, 32 devices: a whole 2x2x4 slice. The times are simulated.
32 devices in a mesh: expert: 16 (over z, y, core), dp: 2 (over x).
Axes of the slice: x: 2, y: 2, z: 4, core: 2. Of those that a mesh axis runs over, the one named last changes fastest.
Arguments:
- tokens: bfloat16 [4096, 2048], P(('dp', 'expert')), parts along dimension 0, may hold values from -6 to 6
- experts_of: int32 [4096, 8], P(('dp', 'expert')), parts along dimension 0, may hold values from 0 to 15, all different within a row; in each aligned block of 128 rows (0 to 127, 128 to 255, ...) at most 80 rows name the same one
- gate_prob: float32 [4096, 8], P(('dp', 'expert')), parts along dimension 0, may hold values from 0.05 to 0.5
- gain: float32 [2048], replicated, may hold values from 0.25 to 1.75
- w_gate_up: bfloat16 [16, 2048, 1536], P('expert'), may hold values from -0.125 to 0.125
- w_down: bfloat16 [16, 768, 2048], P('expert'), may hold values from -0.21875 to 0.21875
Outputs:
- mixed: bfloat16 [4096, 2048], P(('dp', 'expert')), parts along dimension 0
There are 2 independent parts, one for each index of `dp`. A program takes and returns all parts, laid end to end along the dimension named above; an argument that names none is the same for every part. Nothing has to cross between parts.
Inputs may be any that keep to these rules, and one draw needn't show every extreme that they name: `experts_of`: within each token the 8 experts differ; among the rows of one device no expert is named by more than 80 rows, a bound that some block reaches.
All inputs are finite; a program needn't handle non-finite values.
Results may differ from a plain program's by a relative error of at most 0.0052.
Values may be sent and summed in bfloat16 or wider, within the bound.
No kernel may reach another device: no remote copies, remote signals or barrier semaphores. Data moves between devices by JAX's collectives and lax.ppermute only.
A program may use at most 128 MiB of HBM per device.

v0:
```python
import jax
import jax.numpy as jnp
from jax import lax
from jax.sharding import PartitionSpec as P


def expert(rows, proj_in, proj_out):
    units = proj_out.shape[0]
    hidden = jnp.dot(rows, proj_in, preferred_element_type=jnp.float32)
    act = (jax.nn.silu(hidden[:, :units]) * hidden[:, units:]).astype(jnp.bfloat16)
    return jnp.dot(act, proj_out, preferred_element_type=jnp.float32)


def normalize(tokens, gain):
    x_wide = tokens.astype(jnp.float32)
    scale = lax.rsqrt(jnp.mean(x_wide * x_wide, axis=-1, keepdims=True) + 1e-06)
    return (x_wide * scale * gain).astype(jnp.bfloat16)


def gathered(tokens, experts_of, gate_prob, gain, w_gate_up, w_down):
    count = lax.axis_size("expert")
    tok_rows, width = tokens.shape
    half = tok_rows // 2
    wide, narrow = jnp.float32, jnp.bfloat16
    lanes = 3 * count + -3 * count % 128
    lane = lax.broadcasted_iota(jnp.int32, (lanes, 128), 0)
    mine = (lane % count == lax.axis_index("expert")) & (lane < 3 * count)
    mine = mine.astype(narrow)

    def hop(a, s):
        return lax.ppermute(a, "expert", [(i, i ^ s) for i in range(count)])

    def with_gates(normed):
        chosen = experts_of[:, :, None] == jnp.arange(count, dtype=jnp.int32)
        rest = jnp.sum(jnp.where(chosen, gate_prob[:, :, None], 0.0), axis=1)
        terms = []
        for _ in range(3):
            term = lax.reduce_precision(rest, exponent_bits=8, mantissa_bits=7)
            terms.append(term)
            rest = rest - term
        tail = jnp.concatenate(terms, axis=1).astype(narrow)
        tail = jnp.pad(tail, ((0, 0), (0, lanes - tail.shape[1])))
        return jnp.concatenate([normed, tail], axis=1)

    def serve(held):
        pair = held.shape[0]
        other = hop(held, 1)
        rows = jnp.concatenate([held[:, :width], other[:, :width]], axis=0)
        tail = jnp.concatenate([held[:, width:], other[:, width:]], axis=0)
        scale = jnp.dot(tail, mine, preferred_element_type=wide)[:, :1]
        out = (expert(rows, w_gate_up[0], w_down[0]) * scale).astype(narrow)
        got = hop(out[pair:], 1)
        return out[:pair].astype(wide) + got.astype(wide)

    sent = with_gates(normalize(tokens, gain))
    parts = {"a": slice(0, half), "b": slice(half, tok_rows)}
    far = [(d, h) for d in range(count // 4 - 1, 1, -1) for h in parts]
    near = hop(sent, 4)
    across = hop(sent, 2)
    columns = {(d, h): hop(sent[parts[h]], 4 * d) for d, h in far}
    near = jnp.concatenate([near, hop(near, 2)], axis=0)
    own = serve(jnp.concatenate([sent, across], axis=0))
    got = hop(serve(near).astype(narrow), 4)
    own = own + got.astype(wide)

    total = {h: tokens[parts[h]].astype(wide) + own[parts[h]] for h in parts}
    for d, h in far:
        held = jnp.concatenate([columns[d, h], hop(columns[d, h], 2)], axis=0)
        both = serve(held)
        got = hop(both[half:].astype(narrow), 2)
        both = (both[:half] + got.astype(wide)).astype(narrow)
        total[h] = total[h] + hop(both, 4 * d).astype(wide)
    got = hop(own[tok_rows:].astype(narrow), 2).astype(wide)
    return (jnp.concatenate([total["a"], total["b"]], axis=0) + got).astype(narrow)


def exchanged(tokens, experts_of, gate_prob, gain, w_gate_up, w_down):
    count = lax.axis_size("expert")
    tok_rows, width = tokens.shape
    chosen = experts_of.shape[1]
    capacity = (5 * tok_rows * chosen + 4 * count - 1) // (4 * count)
    x_wide = tokens.astype(jnp.float32)
    normed = normalize(tokens, gain)
    flat = experts_of.reshape(-1)
    onehot = (flat[:, None] == jnp.arange(count, dtype=jnp.int32)).astype(jnp.int32)
    rank = jnp.sum((jnp.cumsum(onehot, axis=0) - onehot) * onehot, axis=1)
    slot = flat * capacity + rank
    token_of = jnp.arange(tok_rows * chosen, dtype=jnp.int32) // chosen
    owner = jnp.full((count * capacity,), tok_rows, jnp.int32).at[slot].set(token_of)
    weight_of = jnp.zeros((count * capacity,), jnp.float32).at[slot].set(gate_prob.reshape(-1))
    padded = jnp.concatenate([normed, jnp.zeros((1, width), jnp.bfloat16)], axis=0)
    outgoing = padded[owner].reshape(count, capacity, width)
    rows = lax.all_to_all(outgoing, "expert", split_axis=0, concat_axis=0, tiled=True)
    out_rows = expert(rows.reshape(count * capacity, width), w_gate_up[0], w_down[0])
    out_rows = out_rows.astype(jnp.bfloat16).reshape(count, capacity, width)
    returned = lax.all_to_all(out_rows, "expert", split_axis=0, concat_axis=0, tiled=True)
    returned = returned.reshape(count * capacity, width).astype(jnp.float32)
    total = (
        jnp.zeros((tok_rows + 1, width), jnp.float32).at[owner].add(weight_of[:, None] * returned)
    )
    return (x_wide + total[:tok_rows]).astype(jnp.bfloat16)


def body(tokens, experts_of, *rest):
    count = lax.axis_size("expert")
    dense = count <= 2 * experts_of.shape[1] and count % 8 == 0 and count & (count - 1) == 0
    return (gathered if dense else exchanged)(tokens, experts_of, *rest)


def solution(mesh):
    return jax.shard_map(
        body,
        mesh=mesh,
        in_specs=(
            P(("dp", "expert"), None),
            P(("dp", "expert"), None),
            P(("dp", "expert"), None),
            P(),
            P("expert", None, None),
            P("expert", None, None),
        ),
        out_specs=P(("dp", "expert"), None),
        check_vma=False,
    )
```

profile of v0, /device:TPU:0, one launch (start us, length us, event | category | flops | bytes accessed | tf_op | source)
XLA Modules:
  0.0 176.4 jit_solution(10165448151867449520)
XLA Ops:
  0.0 0.9 select_reduce_fusion
  1.0 1.2 fusion.54
  2.3 1.2 fusion.56
  3.5 1.0 fusion.94
  4.5 4.1 %collective-permute-start.14 = (bf16[64,2176]{1,0:T(8,128)(2,1)}, bf16[64,2176]{1,0:T(8,128)(2,1)}, u32[]{:S(2)}, u32[]{:S(2)}) collective-permute-start(bf16[64,2176]{1,0:T(8,128)(2,1)} %get-tuple-element.7), channel_id=1, source_target_pairs={{0,16},{2,18},{4,20},{6,22},{8,24},{10,26},{12,28},{14,30},{16,0},... | collective-permute-start | bytes 835592 | tf_op jit(solution)/shard_map/ppermute | solution.py:31
  9.4 1.6 collective-permute-start.3
  11.0 1.5 collective-permute-start
  12.7 1.7 collective-permute-start.26
  14.4 8.0 %collective-permute-done.14 = bf16[64,2176]{1,0:T(8,128)(2,1)} collective-permute-done((bf16[64,2176]{1,0:T(8,128)(2,1)}, bf16[64,2176]{1,0:T(8,128)(2,1)}, u32[]{:S(2)}, u32[]{:S(2)}) %collective-permute-start.14) | collective-permute-done | bytes 278560 | tf_op jit(solution)/shard_map/ppermute | solution.py:31
  22.4 2.8 %collective-permute-start.20 = (bf16[64,2176]{1,0:T(8,128)(2,1)}, bf16[64,2176]{1,0:T(8,128)(2,1)S(1)}, u32[]{:S(2)}, u32[]{:S(2)}) collective-permute-start(bf16[64,2176]{1,0:T(8,128)(2,1)} %get-tuple-element.8), channel_id=1, source_target_pairs={{0,24},{2,26},{4,28},{6,30},{8,16},{10,18},{12,20},{14,22},{16,8},... | collective-permute-start | bytes 835592 | tf_op jit(solution)/shard_map/ppermute | solution.py:31
  25.2 1.0 constant_dynamic-update-slice_fusion.5
  26.2 9.6 %collective-permute-done.8 = bf16[64,2176]{1,0:T(8,128)(2,1)} collective-permute-done((bf16[64,2176]{1,0:T(8,128)(2,1)}, bf16[64,2176]{1,0:T(8,128)(2,1)}, u32[]{:S(2)}, u32[]{:S(2)}) %collective-permute-start.8) | collective-permute-done | bytes 278560 | tf_op jit(solution)/shard_map/ppermute | solution.py:31
  35.8 1.5 collective-permute-start.15
  37.3 1.0 constant_dynamic-update-slice_fusion.3
  38.3 13.9 %collective-permute-done.26 = bf16[64,2176]{1,0:T(8,128)(2,1)S(1)} collective-permute-done((bf16[64,2176]{1,0:T(8,128)(2,1)}, bf16[64,2176]{1,0:T(8,128)(2,1)S(1)}, u32[]{:S(2)}, u32[]{:S(2)}) %collective-permute-start.26) | collective-permute-done | bytes 278560 | tf_op jit(solution)/shard_map/ppermute | solution.py:31
  52.2 1.8 %collective-permute-start.9 = (bf16[64,2176]{1,0:T(8,128)(2,1)}, bf16[64,2176]{1,0:T(8,128)(2,1)S(1)}, u32[]{:S(2)}, u32[]{:S(2)}) collective-permute-start(bf16[64,2176]{1,0:T(8,128)(2,1)} %collective-permute-done.8), channel_id=1, source_target_pairs={{0,4},{2,6},{4,0},{6,2},{8,12},{10,14},{12,8},{14,10},{16,20},{18,... | collective-permute-start | bytes 835592 | tf_op jit(solution)/shard_map/ppermute | solution.py:31
  54.3 1.9 %collective-permute-start.21 = (bf16[64,2176]{1,0:T(8,128)(2,1)S(1)}, bf16[64,2176]{1,0:T(8,128)(2,1)S(1)}, u32[]{:S(2)}, u32[]{:S(2)}) collective-permute-start(bf16[64,2176]{1,0:T(8,128)(2,1)S(1)} %collective-permute-done.20), channel_id=1, source_target_pairs={{0,4},{2,6},{4,0},{6,2},{8,12},{10,14},{12,8},{14,10},{16,20},{18,... | collective-permute-start | bytes 835592 | tf_op jit(solution)/shard_map/ppermute | solution.py:31
  56.2 1.3 pad_maximum_fusion
  57.8 4.0 %collective-permute-done.9 = bf16[64,2176]{1,0:T(8,128)(2,1)S(1)} collective-permute-done((bf16[64,2176]{1,0:T(8,128)(2,1)}, bf16[64,2176]{1,0:T(8,128)(2,1)S(1)}, u32[]{:S(2)}, u32[]{:S(2)}) %collective-permute-start.9) | collective-permute-done | bytes 278560 | tf_op jit(solution)/shard_map/ppermute | solution.py:31
  62.0 5.9 %collective-permute-done.27 = bf16[64,2176]{1,0:T(8,128)(2,1)S(1)} collective-permute-done((bf16[64,2176]{1,0:T(8,128)(2,1)S(1)}, bf16[64,2176]{1,0:T(8,128)(2,1)S(1)}, u32[]{:S(2)}, u32[]{:S(2)}) %collective-permute-start.27) | collective-permute-done | bytes 278560 | tf_op jit(solution)/shard_map/ppermute | solution.py:31
  68.5 2.7 %collective-permute-done.21 = bf16[64,2176]{1,0:T(8,128)(2,1)S(1)} collective-permute-done((bf16[64,2176]{1,0:T(8,128)(2,1)S(1)}, bf16[64,2176]{1,0:T(8,128)(2,1)S(1)}, u32[]{:S(2)}, u32[]{:S(2)}) %collective-permute-start.21) | collective-permute-done | bytes 278560 | tf_op jit(solution)/shard_map/ppermute | solution.py:31
  71.3 1.3 collective-permute-start.4
  72.7 1.1 constant_dynamic-update-slice_fusion.1
  73.8 9.8 %collective-permute-done.4 = bf16[128,2176]{1,0:T(8,128)(2,1)S(1)} collective-permute-done((bf16[128,2176]{1,0:T(8,128)(2,1)}, bf16[128,2176]{1,0:T(8,128)(2,1)S(1)}, u32[]{:S(2)}, u32[]{:S(2)}) %collective-permute-start.4) | collective-permute-done | bytes 557088 | tf_op jit(solution)/shard_map/ppermute | solution.py:31
  84.4 1.8 %fusion.4 = f32[256,1536]{1,0:T(8,128)S(1)} fusion(bf16[1,2048,1536]{2,1,0:T(8,128)(2,1)S(1)} %bitcast.49, bf16[128,2048]{1,0:T(8,128)(2,1)S(1)} %slice.325, bf16[128,2048]{1,0:T(8,128)(2,1)S(1)} %slice.324), kind=kOutput, calls=%fused_computation.4 | convolution fusion | flops 1612709888 | bytes 8912896 | tf_op jit(solution)/shard_map/dot_general | solution.py:9
  86.5 1.0 fusion.40
  87.7 1.8 %fusion.6 = f32[256,1536]{1,0:T(8,128)S(1)} fusion(bf16[1,2048,1536]{2,1,0:T(8,128)(2,1)S(1)} %bitcast.49, bf16[128,2048]{1,0:T(8,128)(2,1)S(1)} %slice.315, bf16[128,2048]{1,0:T(8,128)(2,1)S(1)} %slice.314), kind=kOutput, calls=%fused_computation.6 | convolution fusion | flops 1612709888 | bytes 8912896 | tf_op jit(solution)/shard_map/dot_general | solution.py:9
  89.8 1.0 fusion.43
  91.5 1.8 %fusion = f32[256,1536]{1,0:T(8,128)S(1)} fusion(bf16[1,2048,1536]{2,1,0:T(8,128)(2,1)S(1)} %bitcast.49, bf16[128,2048]{1,0:T(8,128)(2,1)S(1)} %slice.348, bf16[128,2048]{1,0:T(8,128)(2,1)S(1)} %slice.347), kind=kOutput, calls=%fused_computation | convolution fusion | flops 1612709888 | bytes 8912896 | tf_op jit(solution)/shard_map/dot_general | solution.py:9
  93.6 1.0 fusion.34
  94.8 1.8 %fusion.2 = f32[256,1536]{1,0:T(8,128)S(1)} fusion(bf16[1,2048,1536]{2,1,0:T(8,128)(2,1)S(1)} %bitcast.49, bf16[128,2048]{1,0:T(8,128)(2,1)S(1)} %slice.338, bf16[128,2048]{1,0:T(8,128)(2,1)S(1)} %slice.337), kind=kOutput, calls=%fused_computation.2 | convolution fusion | flops 1612709888 | bytes 8912896 | tf_op jit(solution)/shard_map/dot_general | solution.py:9
  96.9 1.0 fusion.37
  98.7 1.6 collective-permute-start.18
  101.4 1.6 collective-permute-start.30
  104.2 3.4 %fusion.10 = f32[512,1536]{1,0:T(8,128)S(1)} fusion(bf16[1,2048,1536]{2,1,0:T(8,128)(2,1)S(1)} %bitcast.49, bf16[256,2048]{1,0:T(8,128)(2,1)S(1)} %slice.296, bf16[256,2048]{1,0:T(8,128)(2,1)S(1)} %slice.295), kind=kOutput, calls=%fused_computation.10 | convolution fusion | flops 3225419776 | bytes 11534336 | tf_op jit(solution)/shard_map/dot_general | solution.py:9
  108.0 3.4 %fusion.8 = f32[512,1536]{1,0:T(8,128)S(1)} fusion(bf16[1,2048,1536]{2,1,0:T(8,128)(2,1)S(1)} %bitcast.49, bf16[256,2048]{1,0:T(8,128)(2,1)S(1)} %slice.304, bf16[256,2048]{1,0:T(8,128)(2,1)S(1)} %slice.303), kind=kOutput, calls=%fused_computation.8 | convolution fusion | flops 3225419776 | bytes 11534336 | tf_op jit(solution)/shard_map/dot_general | solution.py:9
  111.4 1.8 %multiply_convert_fusion = bf16[512,2048]{1,0:T(8,128)(2,1)S(1)} fusion(bf16[1,768,2048]{2,1,0:T(8,128)(2,1)S(1)} %copy-done, f32[512]{0:T(512)S(1)} %bitcast.51, f32[512,1536]{1,0:T(8,128)S(1)} %fusion.8), kind=kOutput, calls=%fused_computation.12 | convolution fusion | flops 1615069184 | bytes 8390656 | tf_op jit(solution)/shard_map/dot_general | solution.py:11
  113.5 1.8 %multiply_convert_fusion.1 = bf16[512,2048]{1,0:T(8,128)(2,1)S(1)} fusion(bf16[1,768,2048]{2,1,0:T(8,128)(2,1)S(1)} %copy-done, f32[512]{0:T(512)S(1)} %bitcast.50, f32[512,1536]{1,0:T(8,128)S(1)} %fusion.10), kind=kOutput, calls=%fused_computation.13 | convolution fusion | flops 1615069184 | bytes 8390656 | tf_op jit(solution)/shard_map/dot_general | solution.py:11
  116.1 4.8 %collective-permute-start.19 = (bf16[64,2048]{1,0:T(8,128)(2,1)S(1)}, bf16[64,2048]{1,0:T(8,128)(2,1)S(1)}, u32[]{:S(2)}, u32[]{:S(2)}) collective-permute-start(bf16[64,2048]{1,0:T(8,128)(2,1)S(1)} %fusion.82), channel_id=1, source_target_pairs={{0,16},{2,18},{4,20},{6,22},{8,24},{10,26},{12,28},{14,30},{16,0},... | collective-permute-start | bytes 786440 | tf_op jit(solution)/shard_map/ppermute | solution.py:31
  121.3 1.6 collective-permute-start.7
  123.0 2.0 %collective-permute-start.13 = (bf16[64,2048]{1,0:T(8,128)(2,1)S(1)}, bf16[64,2048]{1,0:T(8,128)(2,1)S(1)}, u32[]{:S(2)}, u32[]{:S(2)}) collective-permute-start(bf16[64,2048]{1,0:T(8,128)(2,1)S(1)} %fusion.83), channel_id=1, source_target_pairs={{0,24},{2,26},{4,28},{6,30},{8,16},{10,18},{12,20},{14,22},{16,8},... | collective-permute-start | bytes 786440 | tf_op jit(solution)/shard_map/ppermute | solution.py:31
  125.1 3.6 %collective-permute-start.31 = (bf16[64,2048]{1,0:T(8,128)(2,1)S(1)}, bf16[64,2048]{1,0:T(8,128)(2,1)S(1)}, u32[]{:S(2)}, u32[]{:S(2)}) collective-permute-start(bf16[64,2048]{1,0:T(8,128)(2,1)S(1)} %fusion.78), channel_id=1, source_target_pairs={{0,16},{2,18},{4,20},{6,22},{8,24},{10,26},{12,28},{14,30},{16,0},... | collective-permute-start | bytes 786440 | tf_op jit(solution)/shard_map/ppermute | solution.py:31
  128.7 1.1 collective-permute-start.25
  129.8 32.5 %collective-permute-done.7 = bf16[256,2048]{1,0:T(8,128)(2,1)S(1)} collective-permute-done((bf16[256,2048]{1,0:T(8,128)(2,1)S(1)}, bf16[256,2048]{1,0:T(8,128)(2,1)S(1)}, u32[]{:S(2)}, u32[]{:S(2)}) %collective-permute-start.7) | collective-permute-done | bytes 1048608 | tf_op jit(solution)/shard_map/ppermute | solution.py:31
  162.9 1.6 collective-permute-start.32
  164.4 3.5 %collective-permute-done.25 = bf16[64,2048]{1,0:T(8,128)(2,1)S(1)} collective-permute-done((bf16[64,2048]{1,0:T(8,128)(2,1)S(1)}, bf16[64,2048]{1,0:T(8,128)(2,1)S(1)}, u32[]{:S(2)}, u32[]{:S(2)}) %collective-permute-start.25) | collective-permute-done | bytes 262176 | tf_op jit(solution)/shard_map/ppermute | solution.py:31
  168.2 7.3 %collective-permute-done.32 = bf16[128,2048]{1,0:T(8,128)(2,1)S(1)} collective-permute-done((bf16[128,2048]{1,0:T(8,128)(2,1)S(1)}, bf16[128,2048]{1,0:T(8,128)(2,1)S(1)}, u32[]{:S(2)}, u32[]{:S(2)}) %collective-permute-start.32) | collective-permute-done | bytes 524320 | tf_op jit(solution)/shard_map/ppermute | solution.py:31
  175.5 0.9 fusion.69
  (119 shorter events, 11.2 us)
Async XLA Ops:
  0.0 86.5 %copy-start = (bf16[1,768,2048]{2,1,0:T(8,128)(2,1)S(1)}, bf16[1,768,2048]{2,1,0:T(8,128)(2,1)}, u32[]{:S(2)}) copy-start(bf16[1,768,2048]{2,1,0:T(8,128)(2,1)} %param.11) | copy-start | bytes 9437188
  3.5 5.1 %copy-start.1 = (bf16[128,2048]{1,0:T(8,128)(2,1)}, bf16[128,2048]{1,0:T(8,128)(2,1)S(1)}, u32[]{:S(2)}) copy-start(bf16[128,2048]{1,0:T(8,128)(2,1)S(1)} %fusion.56) | copy-start | bytes 1572868
  4.5 17.9 %collective-permute-start.14 = (bf16[64,2176]{1,0:T(8,128)(2,1)}, bf16[64,2176]{1,0:T(8,128)(2,1)}, u32[]{:S(2)}, u32[]{:S(2)}) collective-permute-start(bf16[64,2176]{1,0:T(8,128)(2,1)} %get-tuple-element.7), channel_id=1, source_target_pairs={{0,16},{2,18},{4,20},{6,22},{8,24},{10,26},{12,28},{14,30},{16,0},... | collective-permute-start | bytes 835592 | tf_op jit(solution)/shard_map/ppermute | solution.py:31
  9.4 58.5 %collective-permute-start.3 = (bf16[128,2176]{1,0:T(8,128)(2,1)}, bf16[128,2176]{1,0:T(8,128)(2,1)}, u32[]{:S(2)}, u32[]{:S(2)}) collective-permute-start(bf16[128,2176]{1,0:T(8,128)(2,1)} %pad_maximum_fusion.1), channel_id=1, source_target_pairs={{0,8},{2,10},{4,12},{6,14},{8,0},{10,2},{12,4},{14,6},{16,24},{18,... | collective-permute-start | bytes 1671176 | tf_op jit(solution)/shard_map/ppermute | solution.py:31
  11.0 43.3 %collective-permute-start = (bf16[128,2176]{1,0:T(8,128)(2,1)}, bf16[128,2176]{1,0:T(8,128)(2,1)}, u32[]{:S(2)}, u32[]{:S(2)}) collective-permute-start(bf16[128,2176]{1,0:T(8,128)(2,1)} %pad_maximum_fusion.1), channel_id=1, source_target_pairs={{0,4},{2,6},{4,0},{6,2},{8,12},{10,14},{12,8},{14,10},{16,20},{18,... | collective-permute-start | bytes 1671176 | tf_op jit(solution)/shard_map/ppermute | solution.py:31
  12.5 23.2 %collective-permute-start.8 = (bf16[64,2176]{1,0:T(8,128)(2,1)}, bf16[64,2176]{1,0:T(8,128)(2,1)}, u32[]{:S(2)}, u32[]{:S(2)}) collective-permute-start(bf16[64,2176]{1,0:T(8,128)(2,1)} %get-tuple-element.7), channel_id=1, source_target_pairs={{0,24},{2,26},{4,28},{6,30},{8,16},{10,18},{12,20},{14,22},{16,8},... | collective-permute-start | bytes 835592 | tf_op jit(solution)/shard_map/ppermute | solution.py:31
  12.7 39.4 %collective-permute-start.26 = (bf16[64,2176]{1,0:T(8,128)(2,1)}, bf16[64,2176]{1,0:T(8,128)(2,1)S(1)}, u32[]{:S(2)}, u32[]{:S(2)}) collective-permute-start(bf16[64,2176]{1,0:T(8,128)(2,1)} %get-tuple-element.8), channel_id=1, source_target_pairs={{0,16},{2,18},{4,20},{6,22},{8,24},{10,26},{12,28},{14,30},{16,0},... | collective-permute-start | bytes 835592 | tf_op jit(solution)/shard_map/ppermute | solution.py:31
  14.4 41.8 %copy-start.2 = (bf16[128,2048]{1,0:T(8,128)(2,1)S(1)}, bf16[128,2048]{1,0:T(8,128)(2,1)}, u32[]{:S(2)}) copy-start(bf16[128,2048]{1,0:T(8,128)(2,1)} %copy-done.1) | copy-start | bytes 1572868
  22.4 31.6 %collective-permute-start.20 = (bf16[64,2176]{1,0:T(8,128)(2,1)}, bf16[64,2176]{1,0:T(8,128)(2,1)S(1)}, u32[]{:S(2)}, u32[]{:S(2)}) collective-permute-start(bf16[64,2176]{1,0:T(8,128)(2,1)} %get-tuple-element.8), channel_id=1, source_target_pairs={{0,24},{2,26},{4,28},{6,30},{8,16},{10,18},{12,20},{14,22},{16,8},... | collective-permute-start | bytes 835592 | tf_op jit(solution)/shard_map/ppermute | solution.py:31
  35.8 21.9 %collective-permute-start.15 = (bf16[64,2176]{1,0:T(8,128)(2,1)}, bf16[64,2176]{1,0:T(8,128)(2,1)S(1)}, u32[]{:S(2)}, u32[]{:S(2)}) collective-permute-start(bf16[64,2176]{1,0:T(8,128)(2,1)} %collective-permute-done.14), channel_id=1, source_target_pairs={{0,4},{2,6},{4,0},{6,2},{8,12},{10,14},{12,8},{14,10},{16,20},{18,... | collective-permute-start | bytes 835592 | tf_op jit(solution)/shard_map/ppermute | solution.py:31
  52.2 9.7 %collective-permute-start.9 = (bf16[64,2176]{1,0:T(8,128)(2,1)}, bf16[64,2176]{1,0:T(8,128)(2,1)S(1)}, u32[]{:S(2)}, u32[]{:S(2)}) collective-permute-start(bf16[64,2176]{1,0:T(8,128)(2,1)} %collective-permute-done.8), channel_id=1, source_target_pairs={{0,4},{2,6},{4,0},{6,2},{8,12},{10,14},{12,8},{14,10},{16,20},{18,... | collective-permute-start | bytes 835592 | tf_op jit(solution)/shard_map/ppermute | solution.py:31
  54.0 13.8 %collective-permute-start.27 = (bf16[64,2176]{1,0:T(8,128)(2,1)S(1)}, bf16[64,2176]{1,0:T(8,128)(2,1)S(1)}, u32[]{:S(2)}, u32[]{:S(2)}) collective-permute-start(bf16[64,2176]{1,0:T(8,128)(2,1)S(1)} %collective-permute-done.26), channel_id=1, source_target_pairs={{0,4},{2,6},{4,0},{6,2},{8,12},{10,14},{12,8},{14,10},{16,20},{18,... | collective-permute-start | bytes 835592 | tf_op jit(solution)/shard_map/ppermute | solution.py:31
  54.3 17.0 %collective-permute-start.21 = (bf16[64,2176]{1,0:T(8,128)(2,1)S(1)}, bf16[64,2176]{1,0:T(8,128)(2,1)S(1)}, u32[]{:S(2)}, u32[]{:S(2)}) collective-permute-start(bf16[64,2176]{1,0:T(8,128)(2,1)S(1)} %collective-permute-done.20), channel_id=1, source_target_pairs={{0,4},{2,6},{4,0},{6,2},{8,12},{10,14},{12,8},{14,10},{16,20},{18,... | collective-permute-start | bytes 835592 | tf_op jit(solution)/shard_map/ppermute | solution.py:31
  56.2 28.2 %slice-start = ((s8[6291456]{0:T(1024)(128)(4,1)}), s8[4194304]{0:T(1024)(128)(4,1)S(1)}, s32[]{:S(2)}) async-start(s8[6291456]{0:T(1024)(128)(4,1)} %bitcast.48), calls=%async_computation | async-start | bytes 8388608
  57.7 45.5 %collective-permute-start.1 = (bf16[256,2176]{1,0:T(8,128)(2,1)S(1)}, bf16[256,2176]{1,0:T(8,128)(2,1)S(1)}, u32[]{:S(2)}, u32[]{:S(2)}) collective-permute-start(bf16[256,2176]{1,0:T(8,128)(2,1)S(1)} %pad_maximum_fusion), channel_id=1, source_target_pairs={{0,2},{2,0},{4,6},{6,4},{8,10},{10,8},{12,14},{14,12},{16,18},{18,... | collective-permute-start | bytes 3342344 | tf_op jit(solution)/shard_map/ppermute | solution.py:31
  61.9 21.9 %collective-permute-start.16 = (bf16[128,2176]{1,0:T(8,128)(2,1)S(1)}, bf16[128,2176]{1,0:T(8,128)(2,1)S(1)}, u32[]{:S(2)}, u32[]{:S(2)}) collective-permute-start(bf16[128,2176]{1,0:T(8,128)(2,1)S(1)} %constant_dynamic-update-slice_fusion.4), channel_id=1, source_target_pairs={{0,2},{2,0},{4,6},{6,4},{8,10},{10,8},{12,14},{14,12},{16,18},{18,... | collective-permute-start | bytes 1671176 | tf_op jit(solution)/shard_map/ppermute | solution.py:31
  62.0 22.4 %slice-start.1 = ((s8[6291456]{0:T(1024)(128)(4,1)}), s8[2097152]{0:T(1024)(128)(4,1)S(1)}, s32[]{:S(2)}) async-start(s8[6291456]{0:T(1024)(128)(4,1)} %bitcast.48), calls=%async_computation.1 | async-start | bytes 4194304
  67.9 19.7 %collective-permute-start.10 = (bf16[128,2176]{1,0:T(8,128)(2,1)S(1)}, bf16[128,2176]{1,0:T(8,128)(2,1)S(1)}, u32[]{:S(2)}, u32[]{:S(2)}) collective-permute-start(bf16[128,2176]{1,0:T(8,128)(2,1)S(1)} %constant_dynamic-update-slice_fusion.2), channel_id=1, source_target_pairs={{0,2},{2,0},{4,6},{6,4},{8,10},{10,8},{12,14},{14,12},{16,18},{18,... | collective-permute-start | bytes 1671176 | tf_op jit(solution)/shard_map/ppermute | solution.py:31
  68.0 22.9 %collective-permute-start.28 = (bf16[128,2176]{1,0:T(8,128)(2,1)S(1)}, bf16[128,2176]{1,0:T(8,128)(2,1)S(1)}, u32[]{:S(2)}, u32[]{:S(2)}) collective-permute-start(bf16[128,2176]{1,0:T(8,128)(2,1)S(1)} %constant_dynamic-update-slice_fusion.8), channel_id=1, source_target_pairs={{0,2},{2,0},{4,6},{6,4},{8,10},{10,8},{12,14},{14,12},{16,18},{18,... | collective-permute-start | bytes 1671176 | tf_op jit(solution)/shard_map/ppermute | solution.py:31
  71.3 12.3 %collective-permute-start.4 = (bf16[128,2176]{1,0:T(8,128)(2,1)}, bf16[128,2176]{1,0:T(8,128)(2,1)S(1)}, u32[]{:S(2)}, u32[]{:S(2)}) collective-permute-start(bf16[128,2176]{1,0:T(8,128)(2,1)} %collective-permute-done.3), channel_id=1, source_target_pairs={{0,4},{2,6},{4,0},{6,2},{8,12},{10,14},{12,8},{14,10},{16,20},{18,... | collective-permute-start | bytes 1671176 | tf_op jit(solution)/shard_map/ppermute | solution.py:31
  83.6 11.1 %collective-permute-start.22 = (bf16[128,2176]{1,0:T(8,128)(2,1)S(1)}, bf16[128,2176]{1,0:T(8,128)(2,1)S(1)}, u32[]{:S(2)}, u32[]{:S(2)}) collective-permute-start(bf16[128,2176]{1,0:T(8,128)(2,1)S(1)} %constant_dynamic-update-slice_fusion.6), channel_id=1, source_target_pairs={{0,2},{2,0},{4,6},{6,4},{8,10},{10,8},{12,14},{14,12},{16,18},{18,... | collective-permute-start | bytes 1671176 | tf_op jit(solution)/shard_map/ppermute | solution.py:31
  83.8 23.8 %collective-permute-start.5 = (bf16[256,2176]{1,0:T(8,128)(2,1)S(1)}, bf16[256,2176]{1,0:T(8,128)(2,1)S(1)}, u32[]{:S(2)}, u32[]{:S(2)}) collective-permute-start(bf16[256,2176]{1,0:T(8,128)(2,1)S(1)} %constant_dynamic-update-slice_fusion), channel_id=1, source_target_pairs={{0,2},{2,0},{4,6},{6,4},{8,10},{10,8},{12,14},{14,12},{16,18},{18,... | collective-permute-start | bytes 3342344 | tf_op jit(solution)/shard_map/ppermute | solution.py:31
  87.6 10.4 %collective-permute-start.17 = (bf16[128,2048]{1,0:T(8,128)(2,1)S(1)}, bf16[128,2048]{1,0:T(8,128)(2,1)S(1)}, u32[]{:S(2)}, u32[]{:S(2)}) collective-permute-start(bf16[128,2048]{1,0:T(8,128)(2,1)S(1)} %slice.331), channel_id=1, source_target_pairs={{0,2},{2,0},{4,6},{6,4},{8,10},{10,8},{12,14},{14,12},{16,18},{18,... | collective-permute-start | bytes 1572872 | tf_op jit(solution)/shard_map/ppermute | solution.py:31
  90.9 7.8 %collective-permute-start.11 = (bf16[128,2048]{1,0:T(8,128)(2,1)S(1)}, bf16[128,2048]{1,0:T(8,128)(2,1)S(1)}, u32[]{:S(2)}, u32[]{:S(2)}) collective-permute-start(bf16[128,2048]{1,0:T(8,128)(2,1)S(1)} %slice.321), channel_id=1, source_target_pairs={{0,2},{2,0},{4,6},{6,4},{8,10},{10,8},{12,14},{14,12},{16,18},{18,... | collective-permute-start | bytes 1572872 | tf_op jit(solution)/shard_map/ppermute | solution.py:31
  94.7 5.8 %collective-permute-start.29 = (bf16[128,2048]{1,0:T(8,128)(2,1)S(1)}, bf16[128,2048]{1,0:T(8,128)(2,1)S(1)}, u32[]{:S(2)}, u32[]{:S(2)}) collective-permute-start(bf16[128,2048]{1,0:T(8,128)(2,1)S(1)} %slice.354), channel_id=1, source_target_pairs={{0,2},{2,0},{4,6},{6,4},{8,10},{10,8},{12,14},{14,12},{16,18},{18,... | collective-permute-start | bytes 1572872 | tf_op jit(solution)/shard_map/ppermute | solution.py:31
  98.0 3.4 %collective-permute-start.23 = (bf16[128,2048]{1,0:T(8,128)(2,1)S(1)}, bf16[128,2048]{1,0:T(8,128)(2,1)S(1)}, u32[]{:S(2)}, u32[]{:S(2)}) collective-permute-start(bf16[128,2048]{1,0:T(8,128)(2,1)S(1)} %slice.344), channel_id=1, source_target_pairs={{0,2},{2,0},{4,6},{6,4},{8,10},{10,8},{12,14},{14,12},{16,18},{18,... | collective-permute-start | bytes 1572872 | tf_op jit(solution)/shard_map/ppermute | solution.py:31
  98.7 16.7 %collective-permute-start.18 = (bf16[64,2048]{1,0:T(8,128)(2,1)S(1)}, bf16[64,2048]{1,0:T(8,128)(2,1)S(1)}, u32[]{:S(2)}, u32[]{:S(2)}) collective-permute-start(bf16[64,2048]{1,0:T(8,128)(2,1)S(1)} %slice.444), channel_id=1, source_target_pairs={{0,4},{2,6},{4,0},{6,2},{8,12},{10,14},{12,8},{14,10},{16,20},{18,... | collective-permute-start | bytes 786440 | tf_op jit(solution)/shard_map/ppermute | solution.py:31
  100.5 20.8 %collective-permute-start.12 = (bf16[64,2048]{1,0:T(8,128)(2,1)S(1)}, bf16[64,2048]{1,0:T(8,128)(2,1)S(1)}, u32[]{:S(2)}, u32[]{:S(2)}) collective-permute-start(bf16[64,2048]{1,0:T(8,128)(2,1)S(1)} %slice.445), channel_id=1, source_target_pairs={{0,4},{2,6},{4,0},{6,2},{8,12},{10,14},{12,8},{14,10},{16,20},{18,... | collective-permute-start | bytes 786440 | tf_op jit(solution)/shard_map/ppermute | solution.py:31
  101.4 21.6 %collective-permute-start.30 = (bf16[64,2048]{1,0:T(8,128)(2,1)S(1)}, bf16[64,2048]{1,0:T(8,128)(2,1)S(1)}, u32[]{:S(2)}, u32[]{:S(2)}) collective-permute-start(bf16[64,2048]{1,0:T(8,128)(2,1)S(1)} %slice.442), channel_id=1, source_target_pairs={{0,4},{2,6},{4,0},{6,2},{8,12},{10,14},{12,8},{14,10},{16,20},{18,... | collective-permute-start | bytes 786440 | tf_op jit(solution)/shard_map/ppermute | solution.py:31
  103.2 21.9 %collective-permute-start.24 = (bf16[64,2048]{1,0:T(8,128)(2,1)S(1)}, bf16[64,2048]{1,0:T(8,128)(2,1)S(1)}, u32[]{:S(2)}, u32[]{:S(2)}) collective-permute-start(bf16[64,2048]{1,0:T(8,128)(2,1)S(1)} %slice.443), channel_id=1, source_target_pairs={{0,4},{2,6},{4,0},{6,2},{8,12},{10,14},{12,8},{14,10},{16,20},{18,... | collective-permute-start | bytes 786440 | tf_op jit(solution)/shard_map/ppermute | solution.py:31
  113.4 2.7 %collective-permute-start.6 = (bf16[256,2048]{1,0:T(8,128)(2,1)S(1)}, bf16[256,2048]{1,0:T(8,128)(2,1)S(1)}, u32[]{:S(2)}, u32[]{:S(2)}) collective-permute-start(bf16[256,2048]{1,0:T(8,128)(2,1)S(1)} %slice.310), channel_id=1, source_target_pairs={{0,2},{2,0},{4,6},{6,4},{8,10},{10,8},{12,14},{14,12},{16,18},{18,... | collective-permute-start | bytes 3145736 | tf_op jit(solution)/shard_map/ppermute | solution.py:31
  115.4 13.3 %collective-permute-start.2 = (bf16[256,2048]{1,0:T(8,128)(2,1)S(1)}, bf16[256,2048]{1,0:T(8,128)(2,1)S(1)}, u32[]{:S(2)}, u32[]{:S(2)}) collective-permute-start(bf16[256,2048]{1,0:T(8,128)(2,1)S(1)} %slice.302), channel_id=1, source_target_pairs={{0,2},{2,0},{4,6},{6,4},{8,10},{10,8},{12,14},{14,12},{16,18},{18,... | collective-permute-start | bytes 3145736 | tf_op jit(solution)/shard_map/ppermute | solution.py:31
  116.1 48.3 %collective-permute-start.19 = (bf16[64,2048]{1,0:T(8,128)(2,1)S(1)}, bf16[64,2048]{1,0:T(8,128)(2,1)S(1)}, u32[]{:S(2)}, u32[]{:S(2)}) collective-permute-start(bf16[64,2048]{1,0:T(8,128)(2,1)S(1)} %fusion.82), channel_id=1, source_target_pairs={{0,16},{2,18},{4,20},{6,22},{8,24},{10,26},{12,28},{14,30},{16,0},... | collective-permute-start | bytes 786440 | tf_op jit(solution)/shard_map/ppermute | solution.py:31
  121.3 41.0 %collective-permute-start.7 = (bf16[256,2048]{1,0:T(8,128)(2,1)S(1)}, bf16[256,2048]{1,0:T(8,128)(2,1)S(1)}, u32[]{:S(2)}, u32[]{:S(2)}) collective-permute-start(bf16[256,2048]{1,0:T(8,128)(2,1)S(1)} %add_convert_fusion), channel_id=1, source_target_pairs={{0,8},{2,10},{4,12},{6,14},{8,0},{10,2},{12,4},{14,6},{16,24},{18,... | collective-permute-start | bytes 3145736 | tf_op jit(solution)/shard_map/ppermute | solution.py:31
  123.0 41.4 %collective-permute-start.13 = (bf16[64,2048]{1,0:T(8,128)(2,1)S(1)}, bf16[64,2048]{1,0:T(8,128)(2,1)S(1)}, u32[]{:S(2)}, u32[]{:S(2)}) collective-permute-start(bf16[64,2048]{1,0:T(8,128)(2,1)S(1)} %fusion.83), channel_id=1, source_target_pairs={{0,24},{2,26},{4,28},{6,30},{8,16},{10,18},{12,20},{14,22},{16,8},... | collective-permute-start | bytes 786440 | tf_op jit(solution)/shard_map/ppermute | solution.py:31
  125.1 39.4 %collective-permute-start.31 = (bf16[64,2048]{1,0:T(8,128)(2,1)S(1)}, bf16[64,2048]{1,0:T(8,128)(2,1)S(1)}, u32[]{:S(2)}, u32[]{:S(2)}) collective-permute-start(bf16[64,2048]{1,0:T(8,128)(2,1)S(1)} %fusion.78), channel_id=1, source_target_pairs={{0,16},{2,18},{4,20},{6,22},{8,24},{10,26},{12,28},{14,30},{16,0},... | collective-permute-start | bytes 786440 | tf_op jit(solution)/shard_map/ppermute | solution.py:31
  128.7 39.2 %copy-start.3 = (bf16[128,2048]{1,0:T(8,128)(2,1)S(1)}, bf16[128,2048]{1,0:T(8,128)(2,1)}, u32[]{:S(2)}) copy-start(bf16[128,2048]{1,0:T(8,128)(2,1)} %param.6) | copy-start | bytes 1572868
  128.7 39.2 %collective-permute-start.25 = (bf16[64,2048]{1,0:T(8,128)(2,1)S(1)}, bf16[64,2048]{1,0:T(8,128)(2,1)S(1)}, u32[]{:S(2)}, u32[]{:S(2)}) collective-permute-start(bf16[64,2048]{1,0:T(8,128)(2,1)S(1)} %fusion.79), channel_id=1, source_target_pairs={{0,24},{2,26},{4,28},{6,30},{8,16},{10,18},{12,20},{14,22},{16,8},... | collective-permute-start | bytes 786440 | tf_op jit(solution)/shard_map/ppermute | solution.py:31
  162.9 12.6 %collective-permute-start.32 = (bf16[128,2048]{1,0:T(8,128)(2,1)S(1)}, bf16[128,2048]{1,0:T(8,128)(2,1)S(1)}, u32[]{:S(2)}, u32[]{:S(2)}) collective-permute-start(bf16[128,2048]{1,0:T(8,128)(2,1)S(1)} %slice.441), channel_id=1, source_target_pairs={{0,4},{2,6},{4,0},{6,2},{8,12},{10,14},{12,8},{14,10},{16,20},{18,... | collective-permute-start | bytes 1572872 | tf_op jit(solution)/shard_map/ppermute | solution.py:31
where the time goes:
time: 177 us; the launch traced here: 176 us
  waiting for transfers between devices  97.3 us (55%)
  starting transfers between devices  40.8 us (23%)
  matrix products  23.4 us (13%)
  other arithmetic  9.25 us (5%)
  local copies, waits for them, and re-layouts  5 us (3%)
    ppermute x33, waiting for transfers between devices, hop(): return lax.ppermute(a, 'expert', [(i, i ^ s) for i in range(count)])  97.3 us
    ppermute x33, starting transfers between devices, hop(): return lax.ppermute(a, 'expert', [(i, i ^ s) for i in range(count)])  40.8 us
    dot_general x6, matrix products, expert(): hidden = jnp.dot(rows, proj_in, preferred_element_type=jnp.float32)  13.9 us
    dot_general x6, matrix products, expert(): return jnp.dot(act, proj_out, preferred_element_type=jnp.float32)  7.75 us
  transfers between devices with their start and end apart: 33, of which 11 were waited for; matrix products, arithmetic and copies ran while one was open for 18% of the time, Pallas kernels for 0%

commit v1 on v0

--- a/solution.py
+++ b/solution.py
@@ -1,6 +1,9 @@
+import functools
+
 import jax
 import jax.numpy as jnp
 from jax import lax
+from jax.experimental import pallas as pl
 from jax.sharding import PartitionSpec as P
 
 
@@ -17,6 +20,33 @@
     return (x_wide * scale * gain).astype(jnp.bfloat16)
 
 
+def prepare(count, tokens, experts_of, gate_prob, gain, sent, *pieces):
+    rows, width = tokens.shape
+    x_wide = tokens[...].astype(jnp.float32)
+    scale = lax.rsqrt(jnp.mean(x_wide * x_wide, axis=-1, keepdims=True) + 1e-06)
+    normed = (x_wide * scale * gain[...]).astype(jnp.bfloat16)
+    lane = lax.broadcasted_iota(jnp.int32, (sent.shape[1] - width, rows), 0)
+    second, third, spare = lane >= count, lane >= 2 * count, lane >= 3 * count
+    index = jnp.where(third, lane - 2 * count, jnp.where(second, lane - count, lane))
+    rest = jnp.zeros(lane.shape, jnp.float32)
+    for k in range(experts_of.shape[0]):
+        rest += jnp.where(experts_of[k : k + 1, :] == index, gate_prob[k : k + 1, :], 0.0)
+    terms = []
+    for _ in range(3):
+        terms.append(rest.astype(jnp.bfloat16).astype(jnp.float32))
+        rest = rest - terms[-1]
+    tail = jnp.where(third, terms[2], jnp.where(second, terms[1], terms[0]))
+    tail = jnp.where(spare, 0.0, tail).T.astype(jnp.bfloat16)
+    sent[:, :width] = normed
+    sent[:, width:] = tail
+    start = 0
+    for piece in pieces:
+        part = slice(start, start + piece.shape[0])
+        piece[:, :width] = normed[part]
+        piece[:, width:] = tail[part]
+        start = part.stop
+
+
 def gathered(tokens, experts_of, gate_prob, gain, w_gate_up, w_down):
     count = lax.axis_size("expert")
     tok_rows, width = tokens.shape
@@ -30,18 +60,6 @@
     def hop(a, s):
         return lax.ppermute(a, "expert", [(i, i ^ s) for i in range(count)])
 
-    def with_gates(normed):
-        chosen = experts_of[:, :, None] == jnp.arange(count, dtype=jnp.int32)
-        rest = jnp.sum(jnp.where(chosen, gate_prob[:, :, None], 0.0), axis=1)
-        terms = []
-        for _ in range(3):
-            term = lax.reduce_precision(rest, exponent_bits=8, mantissa_bits=7)
-            terms.append(term)
-            rest = rest - term
-        tail = jnp.concatenate(terms, axis=1).astype(narrow)
-        tail = jnp.pad(tail, ((0, 0), (0, lanes - tail.shape[1])))
-        return jnp.concatenate([normed, tail], axis=1)
-
     def serve(held):
         pair = held.shape[0]
         other = hop(held, 1)
@@ -52,12 +70,18 @@
         got = hop(out[pair:], 1)
         return out[:pair].astype(wide) + got.astype(wide)
 
-    sent = with_gates(normalize(tokens, gain))
+    sent, *pieces = pl.pallas_call(
+        functools.partial(prepare, count),
+        out_shape=[
+            jax.ShapeDtypeStruct((rows, width + lanes), narrow) for rows in (tok_rows, half, half)
+        ],
+    )(tokens, experts_of.T, gate_prob.T, gain.reshape(1, -1))
+    pieces = dict(zip("ab", pieces))
     parts = {"a": slice(0, half), "b": slice(half, tok_rows)}
     far = [(d, h) for d in range(count // 4 - 1, 1, -1) for h in parts]
     near = hop(sent, 4)
     across = hop(sent, 2)
-    columns = {(d, h): hop(sent[parts[h]], 4 * d) for d, h in far}
+    columns = {(d, h): hop(pieces[h], 4 * d) for d, h in far}
     near = jnp.concatenate([near, hop(near, 2)], axis=0)
     own = serve(jnp.concatenate([sent, across], axis=0))
     got = hop(serve(near).astype(narrow), 4)

time: 177 us -> 175 us (0.989)
  waiting for transfers between devices: 97.3 us -> 104 us
  other arithmetic: 9.25 us -> 2.76 us
  starting transfers between devices: 40.8 us -> 34.6 us
  Pallas kernels: 0 us -> 2.41 us
  local copies, waits for them, and re-layouts: 5 us -> 7.22 us
    ppermute x33, waiting for transfers between devices: 97.3 us -> 104 us  [hop(): return lax.ppermute(a, 'expert', [(i, i ^ s) for i in range(count)])]
    ppermute x33, starting transfers between devices: 40.8 us -> 34.6 us  [hop(): return lax.ppermute(a, 'expert', [(i, i ^ s) for i in range(count)])]
    concatenate x4 -> x0, other arithmetic: 3.12 us -> none  [the longest x2 1.82 us: with_gates(): return jnp.concatenate([normed, tail], axis=1)]
    pallas_call x0 -> x1, Pallas kernels: none -> 2.41 us  [gathered(): pl.pallas_call(functools.partial(prepare, count), out_shape=[jax.ShapeDty...]
    reduce_sum x2 -> x0, other arithmetic: 2.11 us -> none  [the longest x1 1.24 us: normalize(): scale = lax.rsqrt(jnp.mean(x_wide * x_wide, axis=-1, keepdims=True) + 1e-06)]
    unnamed x18 -> x14, local copies, waits for them, and re-layouts: 3.23 us -> 4.2 us
  transfers between devices with their start and end apart: 33 -> 33, of which waited for: 11 -> 12; matrix products, arithmetic and copies ran while one was open for 18% -> 19% of each run, Pallas kernels for 0% -> 0%
where the time goes in v1:
time: 175 us
  waiting for transfers between devices  104 us (59%)
  starting transfers between devices  34.6 us (20%)
  matrix products  23.4 us (13%)
  local copies, waits for them, and re-layouts  7.22 us (4%)
  other arithmetic  2.76 us (2%)
  Pallas kernels  2.41 us (1%)
    ppermute x33, waiting for transfers between devices, hop(): return lax.ppermute(a, 'expert', [(i, i ^ s) for i in range(count)])  104 us
    ppermute x33, starting transfers between devices, hop(): return lax.ppermute(a, 'expert', [(i, i ^ s) for i in range(count)])  34.6 us
    dot_general x6, matrix products, expert(): hidden = jnp.dot(rows, proj_in, preferred_element_type=jnp.float32)  13.9 us
    dot_general x6, matrix products, expert(): return jnp.dot(act, proj_out, preferred_element_type=jnp.float32)  7.73 us
    unnamed x14, local copies, waits for them, and re-layouts  4.2 us
  transfers between devices with their start and end apart: 33, of which 12 were waited for; matrix products, arithmetic and copies ran while one was open for 19% of the time, Pallas kernels for 0%

profile of v1, /device:TPU:0, one launch (start us, length us, event | category | flops | bytes accessed | tf_op | source)
XLA Modules:
  0.0 175.2 jit_solution(10083527303641212562)
XLA Ops:
  0.0 2.4 %shard_map.64 = (bf16[128,2176]{1,0:T(8,128)(2,1)}, bf16[64,2176]{1,0:T(8,128)(2,1)}, bf16[64,2176]{1,0:T(8,128)(2,1)}) custom-call(bf16[128,2048]{1,0:T(8,128)(2,1)} %tokens.1, s32[8,128]{1,0:T(8,128)} %bitcast.52, f32[8,128]{1,0:T(8,128)} %bitcast.53, f32[1,2048]{1,0:T(1,128)} %bitcast.51), custom_call_target="tpu_custom_call" | custom-call | tf_op jit(solution)/shard_map/pallas_call | solution.py:73
  2.4 3.1 %collective-permute-start.3 = (bf16[128,2176]{1,0:T(8,128)(2,1)}, bf16[128,2176]{1,0:T(8,128)(2,1)}, u32[]{:S(2)}, u32[]{:S(2)}) collective-permute-start(bf16[128,2176]{1,0:T(8,128)(2,1)} %get-tuple-element.8), channel_id=1, source_target_pairs={{0,8},{2,10},{4,12},{6,14},{8,0},{10,2},{12,4},{14,6},{16,24},{18,... | collective-permute-start | bytes 1671176 | tf_op jit(solution)/shard_map/ppermute | solution.py:61
  5.5 1.5 collective-permute-start
  7.0 2.6 %collective-permute-start.14 = (bf16[64,2176]{1,0:T(8,128)(2,1)}, bf16[64,2176]{1,0:T(8,128)(2,1)}, u32[]{:S(2)}, u32[]{:S(2)}) collective-permute-start(bf16[64,2176]{1,0:T(8,128)(2,1)} %get-tuple-element.9), channel_id=1, source_target_pairs={{0,16},{2,18},{4,20},{6,22},{8,24},{10,26},{12,28},{14,30},{16,0},... | collective-permute-start | bytes 835592 | tf_op jit(solution)/shard_map/ppermute | solution.py:61
  9.8 1.7 collective-permute-start.26
  11.5 1.1 constant_dynamic-update-slice_fusion.1
  12.6 12.2 %collective-permute-done.14 = bf16[64,2176]{1,0:T(8,128)(2,1)} collective-permute-done((bf16[64,2176]{1,0:T(8,128)(2,1)}, bf16[64,2176]{1,0:T(8,128)(2,1)}, u32[]{:S(2)}, u32[]{:S(2)}) %collective-permute-start.14) | collective-permute-done | bytes 278560 | tf_op jit(solution)/shard_map/ppermute | solution.py:61
  24.8 2.5 %collective-permute-start.20 = (bf16[64,2176]{1,0:T(8,128)(2,1)}, bf16[64,2176]{1,0:T(8,128)(2,1)S(1)}, u32[]{:S(2)}, u32[]{:S(2)}) collective-permute-start(bf16[64,2176]{1,0:T(8,128)(2,1)} %get-tuple-element.10), channel_id=1, source_target_pairs={{0,24},{2,26},{4,28},{6,30},{8,16},{10,18},{12,20},{14,22},{16,8},... | collective-permute-start | bytes 835592 | tf_op jit(solution)/shard_map/ppermute | solution.py:61
  27.3 1.0 constant_dynamic-update-slice_fusion.7
  28.3 5.5 %collective-permute-done.8 = bf16[64,2176]{1,0:T(8,128)(2,1)} collective-permute-done((bf16[64,2176]{1,0:T(8,128)(2,1)}, bf16[64,2176]{1,0:T(8,128)(2,1)}, u32[]{:S(2)}, u32[]{:S(2)}) %collective-permute-start.8) | collective-permute-done | bytes 278560 | tf_op jit(solution)/shard_map/ppermute | solution.py:61
  33.8 1.5 collective-permute-start.15
  35.3 1.0 constant_dynamic-update-slice_fusion.5
  36.3 17.2 %collective-permute-done.26 = bf16[64,2176]{1,0:T(8,128)(2,1)S(1)} collective-permute-done((bf16[64,2176]{1,0:T(8,128)(2,1)}, bf16[64,2176]{1,0:T(8,128)(2,1)S(1)}, u32[]{:S(2)}, u32[]{:S(2)}) %collective-permute-start.26) | collective-permute-done | bytes 278560 | tf_op jit(solution)/shard_map/ppermute | solution.py:61
  54.0 1.6 collective-permute-start.27
  55.6 0.6 collective-permute-start.21
  56.2 1.3 constant_dynamic-update-slice_fusion
  57.8 5.4 %collective-permute-done.9 = bf16[64,2176]{1,0:T(8,128)(2,1)S(1)} collective-permute-done((bf16[64,2176]{1,0:T(8,128)(2,1)}, bf16[64,2176]{1,0:T(8,128)(2,1)S(1)}, u32[]{:S(2)}, u32[]{:S(2)}) %collective-permute-start.9) | collective-permute-done | bytes 278560 | tf_op jit(solution)/shard_map/ppermute | solution.py:61
  63.3 4.7 %collective-permute-done.27 = bf16[64,2176]{1,0:T(8,128)(2,1)S(1)} collective-permute-done((bf16[64,2176]{1,0:T(8,128)(2,1)S(1)}, bf16[64,2176]{1,0:T(8,128)(2,1)S(1)}, u32[]{:S(2)}, u32[]{:S(2)}) %collective-permute-start.27) | collective-permute-done | bytes 278560 | tf_op jit(solution)/shard_map/ppermute | solution.py:61
  68.1 0.6 collective-permute-start.28
  68.7 2.3 %collective-permute-done.21 = bf16[64,2176]{1,0:T(8,128)(2,1)S(1)} collective-permute-done((bf16[64,2176]{1,0:T(8,128)(2,1)S(1)}, bf16[64,2176]{1,0:T(8,128)(2,1)S(1)}, u32[]{:S(2)}, u32[]{:S(2)}) %collective-permute-start.21) | collective-permute-done | bytes 278560 | tf_op jit(solution)/shard_map/ppermute | solution.py:61
  71.6 1.1 constant_dynamic-update-slice_fusion.3
  72.7 10.8 %collective-permute-done.4 = bf16[128,2176]{1,0:T(8,128)(2,1)S(1)} collective-permute-done((bf16[128,2176]{1,0:T(8,128)(2,1)}, bf16[128,2176]{1,0:T(8,128)(2,1)S(1)}, u32[]{:S(2)}, u32[]{:S(2)}) %collective-permute-start.4) | collective-permute-done | bytes 557088 | tf_op jit(solution)/shard_map/ppermute | solution.py:61
  83.7 0.6 collective-permute-start.5
  84.4 1.8 %fusion.4 = f32[256,1536]{1,0:T(8,128)S(1)} fusion(bf16[1,2048,1536]{2,1,0:T(8,128)(2,1)S(1)} %bitcast.55, bf16[128,2048]{1,0:T(8,128)(2,1)S(1)} %slice.313, bf16[128,2048]{1,0:T(8,128)(2,1)S(1)} %slice.312), kind=kOutput, calls=%fused_computation.4 | convolution fusion | flops 1612709888 | bytes 8912896 | tf_op jit(solution)/shard_map/dot_general | solution.py:12
  86.5 1.0 fusion.40
  87.7 1.8 %fusion.6 = f32[256,1536]{1,0:T(8,128)S(1)} fusion(bf16[1,2048,1536]{2,1,0:T(8,128)(2,1)S(1)} %bitcast.55, bf16[128,2048]{1,0:T(8,128)(2,1)S(1)} %slice.303, bf16[128,2048]{1,0:T(8,128)(2,1)S(1)} %slice.302), kind=kOutput, calls=%fused_computation.6 | convolution fusion | flops 1612709888 | bytes 8912896 | tf_op jit(solution)/shard_map/dot_general | solution.py:12
  89.8 1.0 fusion.43
  91.5 1.8 %fusion = f32[256,1536]{1,0:T(8,128)S(1)} fusion(bf16[1,2048,1536]{2,1,0:T(8,128)(2,1)S(1)} %bitcast.55, bf16[128,2048]{1,0:T(8,128)(2,1)S(1)} %slice.334, bf16[128,2048]{1,0:T(8,128)(2,1)S(1)} %slice.333), kind=kOutput, calls=%fused_computation | convolution fusion | flops 1612709888 | bytes 8912896 | tf_op jit(solution)/shard_map/dot_general | solution.py:12
  93.5 1.0 fusion.34
  94.8 1.8 %fusion.2 = f32[256,1536]{1,0:T(8,128)S(1)} fusion(bf16[1,2048,1536]{2,1,0:T(8,128)(2,1)S(1)} %bitcast.55, bf16[128,2048]{1,0:T(8,128)(2,1)S(1)} %slice.324, bf16[128,2048]{1,0:T(8,128)(2,1)S(1)} %slice.323), kind=kOutput, calls=%fused_computation.2 | convolution fusion | flops 1612709888 | bytes 8912896 | tf_op jit(solution)/shard_map/dot_general | solution.py:12
  96.8 1.0 fusion.37
  98.7 0.6 collective-permute-start.18
  99.4 1.6 collective-permute-start.12
  101.2 0.6 collective-permute-start.30
  102.1 1.6 collective-permute-start.24
  104.1 3.4 %fusion.10 = f32[512,1536]{1,0:T(8,128)S(1)} fusion(bf16[1,2048,1536]{2,1,0:T(8,128)(2,1)S(1)} %bitcast.55, bf16[256,2048]{1,0:T(8,128)(2,1)S(1)} %slice.286, bf16[256,2048]{1,0:T(8,128)(2,1)S(1)} %slice.285), kind=kOutput, calls=%fused_computation.10 | convolution fusion | flops 3225419776 | bytes 11534336 | tf_op jit(solution)/shard_map/dot_general | solution.py:12
  108.0 3.4 %fusion.8 = f32[512,1536]{1,0:T(8,128)S(1)} fusion(bf16[1,2048,1536]{2,1,0:T(8,128)(2,1)S(1)} %bitcast.55, bf16[256,2048]{1,0:T(8,128)(2,1)S(1)} %slice.294, bf16[256,2048]{1,0:T(8,128)(2,1)S(1)} %slice.293), kind=kOutput, calls=%fused_computation.8 | convolution fusion | flops 3225419776 | bytes 11534336 | tf_op jit(solution)/shard_map/dot_general | solution.py:12
  111.4 1.8 %multiply_convert_fusion = bf16[512,2048]{1,0:T(8,128)(2,1)S(1)} fusion(bf16[1,768,2048]{2,1,0:T(8,128)(2,1)S(1)} %copy-done, f32[512]{0:T(512)S(1)} %bitcast.57, f32[512,1536]{1,0:T(8,128)S(1)} %fusion.8), kind=kOutput, calls=%fused_computation.12 | convolution fusion | flops 1615069184 | bytes 8390656 | tf_op jit(solution)/shard_map/dot_general | solution.py:14
  113.4 1.8 %multiply_convert_fusion.1 = bf16[512,2048]{1,0:T(8,128)(2,1)S(1)} fusion(bf16[1,768,2048]{2,1,0:T(8,128)(2,1)S(1)} %copy-done, f32[512]{0:T(512)S(1)} %bitcast.56, f32[512,1536]{1,0:T(8,128)S(1)} %fusion.10), kind=kOutput, calls=%fused_computation.13 | convolution fusion | flops 1615069184 | bytes 8390656 | tf_op jit(solution)/shard_map/dot_general | solution.py:14
  116.0 3.7 %collective-permute-start.19 = (bf16[64,2048]{1,0:T(8,128)(2,1)S(1)}, bf16[64,2048]{1,0:T(8,128)(2,1)S(1)}, u32[]{:S(2)}, u32[]{:S(2)}) collective-permute-start(bf16[64,2048]{1,0:T(8,128)(2,1)S(1)} %fusion.79), channel_id=1, source_target_pairs={{0,16},{2,18},{4,20},{6,22},{8,24},{10,26},{12,28},{14,30},{16,0},... | collective-permute-start | bytes 786440 | tf_op jit(solution)/shard_map/ppermute | solution.py:61
  120.3 1.5 collective-permute-start.13
  121.8 2.0 %collective-permute-done.24 = bf16[64,2048]{1,0:T(8,128)(2,1)S(1)} collective-permute-done((bf16[64,2048]{1,0:T(8,128)(2,1)S(1)}, bf16[64,2048]{1,0:T(8,128)(2,1)S(1)}, u32[]{:S(2)}, u32[]{:S(2)}) %collective-permute-start.24) | collective-permute-done | bytes 262176 | tf_op jit(solution)/shard_map/ppermute | solution.py:61
  123.8 3.7 %collective-permute-start.31 = (bf16[64,2048]{1,0:T(8,128)(2,1)S(1)}, bf16[64,2048]{1,0:T(8,128)(2,1)S(1)}, u32[]{:S(2)}, u32[]{:S(2)}) collective-permute-start(bf16[64,2048]{1,0:T(8,128)(2,1)S(1)} %fusion.75), channel_id=1, source_target_pairs={{0,16},{2,18},{4,20},{6,22},{8,24},{10,26},{12,28},{14,30},{16,0},... | collective-permute-start | bytes 786440 | tf_op jit(solution)/shard_map/ppermute | solution.py:61
  127.6 1.4 collective-permute-start.25
  129.0 32.3 %collective-permute-done.7 = bf16[256,2048]{1,0:T(8,128)(2,1)S(1)} collective-permute-done((bf16[256,2048]{1,0:T(8,128)(2,1)S(1)}, bf16[256,2048]{1,0:T(8,128)(2,1)S(1)}, u32[]{:S(2)}, u32[]{:S(2)}) %collective-permute-start.7) | collective-permute-done | bytes 1048608 | tf_op jit(solution)/shard_map/ppermute | solution.py:61
  162.4 4.4 %collective-permute-done.25 = bf16[64,2048]{1,0:T(8,128)(2,1)S(1)} collective-permute-done((bf16[64,2048]{1,0:T(8,128)(2,1)S(1)}, bf16[64,2048]{1,0:T(8,128)(2,1)S(1)}, u32[]{:S(2)}, u32[]{:S(2)}) %collective-permute-start.25) | collective-permute-done | bytes 262176 | tf_op jit(solution)/shard_map/ppermute | solution.py:61
  167.1 7.2 %collective-permute-done.32 = bf16[128,2048]{1,0:T(8,128)(2,1)S(1)} collective-permute-done((bf16[128,2048]{1,0:T(8,128)(2,1)S(1)}, bf16[128,2048]{1,0:T(8,128)(2,1)S(1)}, u32[]{:S(2)}, u32[]{:S(2)}) %collective-permute-start.32) | collective-permute-done | bytes 524320 | tf_op jit(solution)/shard_map/ppermute | solution.py:61
  174.3 0.9 fusion.66
  (107 shorter events, 9.4 us)
Async XLA Ops:
  0.0 86.5 %copy-start = (bf16[1,768,2048]{2,1,0:T(8,128)(2,1)S(1)}, bf16[1,768,2048]{2,1,0:T(8,128)(2,1)}, u32[]{:S(2)}) copy-start(bf16[1,768,2048]{2,1,0:T(8,128)(2,1)} %param.11) | copy-start | bytes 9437188
  2.4 65.7 %collective-permute-start.3 = (bf16[128,2176]{1,0:T(8,128)(2,1)}, bf16[128,2176]{1,0:T(8,128)(2,1)}, u32[]{:S(2)}, u32[]{:S(2)}) collective-permute-start(bf16[128,2176]{1,0:T(8,128)(2,1)} %get-tuple-element.8), channel_id=1, source_target_pairs={{0,8},{2,10},{4,12},{6,14},{8,0},{10,2},{12,4},{14,6},{16,24},{18,... | collective-permute-start | bytes 1671176 | tf_op jit(solution)/shard_map/ppermute | solution.py:61
  5.5 50.1 %collective-permute-start = (bf16[128,2176]{1,0:T(8,128)(2,1)}, bf16[128,2176]{1,0:T(8,128)(2,1)}, u32[]{:S(2)}, u32[]{:S(2)}) collective-permute-start(bf16[128,2176]{1,0:T(8,128)(2,1)} %get-tuple-element.8), channel_id=1, source_target_pairs={{0,4},{2,6},{4,0},{6,2},{8,12},{10,14},{12,8},{14,10},{16,20},{18,... | collective-permute-start | bytes 1671176 | tf_op jit(solution)/shard_map/ppermute | solution.py:61
  7.0 17.8 %collective-permute-start.14 = (bf16[64,2176]{1,0:T(8,128)(2,1)}, bf16[64,2176]{1,0:T(8,128)(2,1)}, u32[]{:S(2)}, u32[]{:S(2)}) collective-permute-start(bf16[64,2176]{1,0:T(8,128)(2,1)} %get-tuple-element.9), channel_id=1, source_target_pairs={{0,16},{2,18},{4,20},{6,22},{8,24},{10,26},{12,28},{14,30},{16,0},... | collective-permute-start | bytes 835592 | tf_op jit(solution)/shard_map/ppermute | solution.py:61
  9.6 24.2 %collective-permute-start.8 = (bf16[64,2176]{1,0:T(8,128)(2,1)}, bf16[64,2176]{1,0:T(8,128)(2,1)}, u32[]{:S(2)}, u32[]{:S(2)}) collective-permute-start(bf16[64,2176]{1,0:T(8,128)(2,1)} %get-tuple-element.9), channel_id=1, source_target_pairs={{0,24},{2,26},{4,28},{6,30},{8,16},{10,18},{12,20},{14,22},{16,8},... | collective-permute-start | bytes 835592 | tf_op jit(solution)/shard_map/ppermute | solution.py:61
  9.8 43.6 %collective-permute-start.26 = (bf16[64,2176]{1,0:T(8,128)(2,1)}, bf16[64,2176]{1,0:T(8,128)(2,1)S(1)}, u32[]{:S(2)}, u32[]{:S(2)}) collective-permute-start(bf16[64,2176]{1,0:T(8,128)(2,1)} %get-tuple-element.10), channel_id=1, source_target_pairs={{0,16},{2,18},{4,20},{6,22},{8,24},{10,26},{12,28},{14,30},{16,0},... | collective-permute-start | bytes 835592 | tf_op jit(solution)/shard_map/ppermute | solution.py:61
  24.8 29.2 %collective-permute-start.20 = (bf16[64,2176]{1,0:T(8,128)(2,1)}, bf16[64,2176]{1,0:T(8,128)(2,1)S(1)}, u32[]{:S(2)}, u32[]{:S(2)}) collective-permute-start(bf16[64,2176]{1,0:T(8,128)(2,1)} %get-tuple-element.10), channel_id=1, source_target_pairs={{0,24},{2,26},{4,28},{6,30},{8,16},{10,18},{12,20},{14,22},{16,8},... | collective-permute-start | bytes 835592 | tf_op jit(solution)/shard_map/ppermute | solution.py:61
  33.8 23.8 %collective-permute-start.15 = (bf16[64,2176]{1,0:T(8,128)(2,1)}, bf16[64,2176]{1,0:T(8,128)(2,1)S(1)}, u32[]{:S(2)}, u32[]{:S(2)}) collective-permute-start(bf16[64,2176]{1,0:T(8,128)(2,1)} %collective-permute-done.14), channel_id=1, source_target_pairs={{0,4},{2,6},{4,0},{6,2},{8,12},{10,14},{12,8},{14,10},{16,20},{18,... | collective-permute-start | bytes 835592 | tf_op jit(solution)/shard_map/ppermute | solution.py:61
  53.4 9.7 %collective-permute-start.9 = (bf16[64,2176]{1,0:T(8,128)(2,1)}, bf16[64,2176]{1,0:T(8,128)(2,1)S(1)}, u32[]{:S(2)}, u32[]{:S(2)}) collective-permute-start(bf16[64,2176]{1,0:T(8,128)(2,1)} %collective-permute-done.8), channel_id=1, source_target_pairs={{0,4},{2,6},{4,0},{6,2},{8,12},{10,14},{12,8},{14,10},{16,20},{18,... | collective-permute-start | bytes 835592 | tf_op jit(solution)/shard_map/ppermute | solution.py:61
  54.0 14.0 %collective-permute-start.27 = (bf16[64,2176]{1,0:T(8,128)(2,1)S(1)}, bf16[64,2176]{1,0:T(8,128)(2,1)S(1)}, u32[]{:S(2)}, u32[]{:S(2)}) collective-permute-start(bf16[64,2176]{1,0:T(8,128)(2,1)S(1)} %collective-permute-done.26), channel_id=1, source_target_pairs={{0,4},{2,6},{4,0},{6,2},{8,12},{10,14},{12,8},{14,10},{16,20},{18,... | collective-permute-start | bytes 835592 | tf_op jit(solution)/shard_map/ppermute | solution.py:61
  55.6 15.4 %collective-permute-start.21 = (bf16[64,2176]{1,0:T(8,128)(2,1)S(1)}, bf16[64,2176]{1,0:T(8,128)(2,1)S(1)}, u32[]{:S(2)}, u32[]{:S(2)}) collective-permute-start(bf16[64,2176]{1,0:T(8,128)(2,1)S(1)} %collective-permute-done.20), channel_id=1, source_target_pairs={{0,4},{2,6},{4,0},{6,2},{8,12},{10,14},{12,8},{14,10},{16,20},{18,... | collective-permute-start | bytes 835592 | tf_op jit(solution)/shard_map/ppermute | solution.py:61
  56.2 28.2 %slice-start = ((s8[6291456]{0:T(1024)(128)(4,1)}), s8[4194304]{0:T(1024)(128)(4,1)S(1)}, s32[]{:S(2)}) async-start(s8[6291456]{0:T(1024)(128)(4,1)} %bitcast.54), calls=%async_computation | async-start | bytes 8388608
  57.6 44.5 %collective-permute-start.1 = (bf16[256,2176]{1,0:T(8,128)(2,1)S(1)}, bf16[256,2176]{1,0:T(8,128)(2,1)S(1)}, u32[]{:S(2)}, u32[]{:S(2)}) collective-permute-start(bf16[256,2176]{1,0:T(8,128)(2,1)S(1)} %constant_dynamic-update-slice_fusion), channel_id=1, source_target_pairs={{0,2},{2,0},{4,6},{6,4},{8,10},{10,8},{12,14},{14,12},{16,18},{18,... | collective-permute-start | bytes 3342344 | tf_op jit(solution)/shard_map/ppermute | solution.py:61
  63.2 20.5 %collective-permute-start.16 = (bf16[128,2176]{1,0:T(8,128)(2,1)S(1)}, bf16[128,2176]{1,0:T(8,128)(2,1)S(1)}, u32[]{:S(2)}, u32[]{:S(2)}) collective-permute-start(bf16[128,2176]{1,0:T(8,128)(2,1)S(1)} %constant_dynamic-update-slice_fusion.6), channel_id=1, source_target_pairs={{0,2},{2,0},{4,6},{6,4},{8,10},{10,8},{12,14},{14,12},{16,18},{18,... | collective-permute-start | bytes 1671176 | tf_op jit(solution)/shard_map/ppermute | solution.py:61
  68.0 19.6 %collective-permute-start.10 = (bf16[128,2176]{1,0:T(8,128)(2,1)S(1)}, bf16[128,2176]{1,0:T(8,128)(2,1)S(1)}, u32[]{:S(2)}, u32[]{:S(2)}) collective-permute-start(bf16[128,2176]{1,0:T(8,128)(2,1)S(1)} %constant_dynamic-update-slice_fusion.4), channel_id=1, source_target_pairs={{0,2},{2,0},{4,6},{6,4},{8,10},{10,8},{12,14},{14,12},{16,18},{18,... | collective-permute-start | bytes 1671176 | tf_op jit(solution)/shard_map/ppermute | solution.py:61
  68.0 16.3 %slice-start.1 = ((s8[6291456]{0:T(1024)(128)(4,1)}), s8[2097152]{0:T(1024)(128)(4,1)S(1)}, s32[]{:S(2)}) async-start(s8[6291456]{0:T(1024)(128)(4,1)} %bitcast.54), calls=%async_computation.1 | async-start | bytes 4194304
  68.1 22.7 %collective-permute-start.28 = (bf16[128,2176]{1,0:T(8,128)(2,1)S(1)}, bf16[128,2176]{1,0:T(8,128)(2,1)S(1)}, u32[]{:S(2)}, u32[]{:S(2)}) collective-permute-start(bf16[128,2176]{1,0:T(8,128)(2,1)S(1)} %constant_dynamic-update-slice_fusion.10), channel_id=1, source_target_pairs={{0,2},{2,0},{4,6},{6,4},{8,10},{10,8},{12,14},{14,12},{16,18},{18,... | collective-permute-start | bytes 1671176 | tf_op jit(solution)/shard_map/ppermute | solution.py:61
  71.0 12.5 %collective-permute-start.4 = (bf16[128,2176]{1,0:T(8,128)(2,1)}, bf16[128,2176]{1,0:T(8,128)(2,1)S(1)}, u32[]{:S(2)}, u32[]{:S(2)}) collective-permute-start(bf16[128,2176]{1,0:T(8,128)(2,1)} %collective-permute-done.3), channel_id=1, source_target_pairs={{0,4},{2,6},{4,0},{6,2},{8,12},{10,14},{12,8},{14,10},{16,20},{18,... | collective-permute-start | bytes 1671176 | tf_op jit(solution)/shard_map/ppermute | solution.py:61
  83.5 11.1 %collective-permute-start.22 = (bf16[128,2176]{1,0:T(8,128)(2,1)S(1)}, bf16[128,2176]{1,0:T(8,128)(2,1)S(1)}, u32[]{:S(2)}, u32[]{:S(2)}) collective-permute-start(bf16[128,2176]{1,0:T(8,128)(2,1)S(1)} %constant_dynamic-update-slice_fusion.8), channel_id=1, source_target_pairs={{0,2},{2,0},{4,6},{6,4},{8,10},{10,8},{12,14},{14,12},{16,18},{18,... | collective-permute-start | bytes 1671176 | tf_op jit(solution)/shard_map/ppermute | solution.py:61
  83.7 23.8 %collective-permute-start.5 = (bf16[256,2176]{1,0:T(8,128)(2,1)S(1)}, bf16[256,2176]{1,0:T(8,128)(2,1)S(1)}, u32[]{:S(2)}, u32[]{:S(2)}) collective-permute-start(bf16[256,2176]{1,0:T(8,128)(2,1)S(1)} %constant_dynamic-update-slice_fusion.2), channel_id=1, source_target_pairs={{0,2},{2,0},{4,6},{6,4},{8,10},{10,8},{12,14},{14,12},{16,18},{18,... | collective-permute-start | bytes 3342344 | tf_op jit(solution)/shard_map/ppermute | solution.py:61
  87.5 10.4 %collective-permute-start.17 = (bf16[128,2048]{1,0:T(8,128)(2,1)S(1)}, bf16[128,2048]{1,0:T(8,128)(2,1)S(1)}, u32[]{:S(2)}, u32[]{:S(2)}) collective-permute-start(bf16[128,2048]{1,0:T(8,128)(2,1)S(1)} %slice.319), channel_id=1, source_target_pairs={{0,2},{2,0},{4,6},{6,4},{8,10},{10,8},{12,14},{14,12},{16,18},{18,... | collective-permute-start | bytes 1572872 | tf_op jit(solution)/shard_map/ppermute | solution.py:61
  90.8 7.8 %collective-permute-start.11 = (bf16[128,2048]{1,0:T(8,128)(2,1)S(1)}, bf16[128,2048]{1,0:T(8,128)(2,1)S(1)}, u32[]{:S(2)}, u32[]{:S(2)}) collective-permute-start(bf16[128,2048]{1,0:T(8,128)(2,1)S(1)} %slice.309), channel_id=1, source_target_pairs={{0,2},{2,0},{4,6},{6,4},{8,10},{10,8},{12,14},{14,12},{16,18},{18,... | collective-permute-start | bytes 1572872 | tf_op jit(solution)/shard_map/ppermute | solution.py:61
  94.6 4.8 %collective-permute-start.29 = (bf16[128,2048]{1,0:T(8,128)(2,1)S(1)}, bf16[128,2048]{1,0:T(8,128)(2,1)S(1)}, u32[]{:S(2)}, u32[]{:S(2)}) collective-permute-start(bf16[128,2048]{1,0:T(8,128)(2,1)S(1)} %slice.340), channel_id=1, source_target_pairs={{0,2},{2,0},{4,6},{6,4},{8,10},{10,8},{12,14},{14,12},{16,18},{18,... | collective-permute-start | bytes 1572872 | tf_op jit(solution)/shard_map/ppermute | solution.py:61
  97.9 3.2 %collective-permute-start.23 = (bf16[128,2048]{1,0:T(8,128)(2,1)S(1)}, bf16[128,2048]{1,0:T(8,128)(2,1)S(1)}, u32[]{:S(2)}, u32[]{:S(2)}) collective-permute-start(bf16[128,2048]{1,0:T(8,128)(2,1)S(1)} %slice.330), channel_id=1, source_target_pairs={{0,2},{2,0},{4,6},{6,4},{8,10},{10,8},{12,14},{14,12},{16,18},{18,... | collective-permute-start | bytes 1572872 | tf_op jit(solution)/shard_map/ppermute | solution.py:61
  98.7 16.7 %collective-permute-start.18 = (bf16[64,2048]{1,0:T(8,128)(2,1)S(1)}, bf16[64,2048]{1,0:T(8,128)(2,1)S(1)}, u32[]{:S(2)}, u32[]{:S(2)}) collective-permute-start(bf16[64,2048]{1,0:T(8,128)(2,1)S(1)} %slice.418), channel_id=1, source_target_pairs={{0,4},{2,6},{4,0},{6,2},{8,12},{10,14},{12,8},{14,10},{16,20},{18,... | collective-permute-start | bytes 786440 | tf_op jit(solution)/shard_map/ppermute | solution.py:61
  99.4 20.7 %collective-permute-start.12 = (bf16[64,2048]{1,0:T(8,128)(2,1)S(1)}, bf16[64,2048]{1,0:T(8,128)(2,1)S(1)}, u32[]{:S(2)}, u32[]{:S(2)}) collective-permute-start(bf16[64,2048]{1,0:T(8,128)(2,1)S(1)} %slice.419), channel_id=1, source_target_pairs={{0,4},{2,6},{4,0},{6,2},{8,12},{10,14},{12,8},{14,10},{16,20},{18,... | collective-permute-start | bytes 786440 | tf_op jit(solution)/shard_map/ppermute | solution.py:61
  101.2 19.1 %collective-permute-start.30 = (bf16[64,2048]{1,0:T(8,128)(2,1)S(1)}, bf16[64,2048]{1,0:T(8,128)(2,1)S(1)}, u32[]{:S(2)}, u32[]{:S(2)}) collective-permute-start(bf16[64,2048]{1,0:T(8,128)(2,1)S(1)} %slice.416), channel_id=1, source_target_pairs={{0,4},{2,6},{4,0},{6,2},{8,12},{10,14},{12,8},{14,10},{16,20},{18,... | collective-permute-start | bytes 786440 | tf_op jit(solution)/shard_map/ppermute | solution.py:61
  102.1 21.7 %collective-permute-start.24 = (bf16[64,2048]{1,0:T(8,128)(2,1)S(1)}, bf16[64,2048]{1,0:T(8,128)(2,1)S(1)}, u32[]{:S(2)}, u32[]{:S(2)}) collective-permute-start(bf16[64,2048]{1,0:T(8,128)(2,1)S(1)} %slice.417), channel_id=1, source_target_pairs={{0,4},{2,6},{4,0},{6,2},{8,12},{10,14},{12,8},{14,10},{16,20},{18,... | collective-permute-start | bytes 786440 | tf_op jit(solution)/shard_map/ppermute | solution.py:61
  113.3 2.7 %collective-permute-start.6 = (bf16[256,2048]{1,0:T(8,128)(2,1)S(1)}, bf16[256,2048]{1,0:T(8,128)(2,1)S(1)}, u32[]{:S(2)}, u32[]{:S(2)}) collective-permute-start(bf16[256,2048]{1,0:T(8,128)(2,1)S(1)} %slice.300), channel_id=1, source_target_pairs={{0,2},{2,0},{4,6},{6,4},{8,10},{10,8},{12,14},{14,12},{16,18},{18,... | collective-permute-start | bytes 3145736 | tf_op jit(solution)/shard_map/ppermute | solution.py:61
  115.3 12.2 %collective-permute-start.2 = (bf16[256,2048]{1,0:T(8,128)(2,1)S(1)}, bf16[256,2048]{1,0:T(8,128)(2,1)S(1)}, u32[]{:S(2)}, u32[]{:S(2)}) collective-permute-start(bf16[256,2048]{1,0:T(8,128)(2,1)S(1)} %slice.292), channel_id=1, source_target_pairs={{0,2},{2,0},{4,6},{6,4},{8,10},{10,8},{12,14},{14,12},{16,18},{18,... | collective-permute-start | bytes 3145736 | tf_op jit(solution)/shard_map/ppermute | solution.py:61
  116.0 46.3 %collective-permute-start.19 = (bf16[64,2048]{1,0:T(8,128)(2,1)S(1)}, bf16[64,2048]{1,0:T(8,128)(2,1)S(1)}, u32[]{:S(2)}, u32[]{:S(2)}) collective-permute-start(bf16[64,2048]{1,0:T(8,128)(2,1)S(1)} %fusion.79), channel_id=1, source_target_pairs={{0,16},{2,18},{4,20},{6,22},{8,24},{10,26},{12,28},{14,30},{16,0},... | collective-permute-start | bytes 786440 | tf_op jit(solution)/shard_map/ppermute | solution.py:61
  120.1 41.1 %collective-permute-start.7 = (bf16[256,2048]{1,0:T(8,128)(2,1)S(1)}, bf16[256,2048]{1,0:T(8,128)(2,1)S(1)}, u32[]{:S(2)}, u32[]{:S(2)}) collective-permute-start(bf16[256,2048]{1,0:T(8,128)(2,1)S(1)} %add_convert_fusion), channel_id=1, source_target_pairs={{0,8},{2,10},{4,12},{6,14},{8,0},{10,2},{12,4},{14,6},{16,24},{18,... | collective-permute-start | bytes 3145736 | tf_op jit(solution)/shard_map/ppermute | solution.py:61
  120.3 42.1 %collective-permute-start.13 = (bf16[64,2048]{1,0:T(8,128)(2,1)S(1)}, bf16[64,2048]{1,0:T(8,128)(2,1)S(1)}, u32[]{:S(2)}, u32[]{:S(2)}) collective-permute-start(bf16[64,2048]{1,0:T(8,128)(2,1)S(1)} %fusion.80), channel_id=1, source_target_pairs={{0,24},{2,26},{4,28},{6,30},{8,16},{10,18},{12,20},{14,22},{16,8},... | collective-permute-start | bytes 786440 | tf_op jit(solution)/shard_map/ppermute | solution.py:61
  123.8 38.6 %collective-permute-start.31 = (bf16[64,2048]{1,0:T(8,128)(2,1)S(1)}, bf16[64,2048]{1,0:T(8,128)(2,1)S(1)}, u32[]{:S(2)}, u32[]{:S(2)}) collective-permute-start(bf16[64,2048]{1,0:T(8,128)(2,1)S(1)} %fusion.75), channel_id=1, source_target_pairs={{0,16},{2,18},{4,20},{6,22},{8,24},{10,26},{12,28},{14,30},{16,0},... | collective-permute-start | bytes 786440 | tf_op jit(solution)/shard_map/ppermute | solution.py:61
  127.5 39.3 %copy-start.1 = (bf16[128,2048]{1,0:T(8,128)(2,1)S(1)}, bf16[128,2048]{1,0:T(8,128)(2,1)}, u32[]{:S(2)}) copy-start(bf16[128,2048]{1,0:T(8,128)(2,1)} %tokens.1) | copy-start | bytes 1572868
  127.6 39.2 %collective-permute-start.25 = (bf16[64,2048]{1,0:T(8,128)(2,1)S(1)}, bf16[64,2048]{1,0:T(8,128)(2,1)S(1)}, u32[]{:S(2)}, u32[]{:S(2)}) collective-permute-start(bf16[64,2048]{1,0:T(8,128)(2,1)S(1)} %fusion.76), channel_id=1, source_target_pairs={{0,24},{2,26},{4,28},{6,30},{8,16},{10,18},{12,20},{14,22},{16,8},... | collective-permute-start | bytes 786440 | tf_op jit(solution)/shard_map/ppermute | solution.py:61
  161.8 12.5 %collective-permute-start.32 = (bf16[128,2048]{1,0:T(8,128)(2,1)S(1)}, bf16[128,2048]{1,0:T(8,128)(2,1)S(1)}, u32[]{:S(2)}, u32[]{:S(2)}) collective-permute-start(bf16[128,2048]{1,0:T(8,128)(2,1)S(1)} %slice.415), channel_id=1, source_target_pairs={{0,4},{2,6},{4,0},{6,2},{8,12},{10,14},{12,8},{14,10},{16,20},{18,... | collective-permute-start | bytes 1572872 | tf_op jit(solution)/shard_map/ppermute | solution.py:61
